TPU v7x, 32 devices: a whole 2x2x4 slice. The times are simulated.
32 devices in a mesh: gx: 4 (over x, core), gy: 2 (over y), gz: 4 (over z).
Axes of the slice: x: 2, y: 2, z: 4, core: 2. Of those that a mesh axis runs over, the one named last changes fastest.
Arguments:
- opening_warmth_field: float32 [32, 32, 512], P('gx', 'gy', 'gz'), may hold values from -42 to 42
- cellwise_warming_source: float32 [32, 32, 512], P('gx', 'gy', 'gz'), may hold values from -6 to 6
- substance_category_per_voxel: int32 [32, 32, 512], P('gx', 'gy', 'gz'), may hold values from 0 to 15
- thermal_coefficient_table: float32 [16], replicated, may hold values from 0.2 to 5
- boundary_cooling_flags: int32 [32, 32, 512], P('gx', 'gy', 'gz'), may hold values 0 or 1
Outputs:
- closing_warmth_field: float32 [32, 32, 512], P('gx', 'gy', 'gz')
- remaining_mismatch: float32 [32, 32, 512], P('gx', 'gy', 'gz')
All inputs are finite; a program needn't handle non-finite values. No bound on the sum of `boundary_cooling_flags` on one device may be relied on, other than what follows from the above.
Results may differ from a plain program's by a relative error of at most 0.00055.
Values sent between devices are 32-bit elements; how exact they have to be, the bound alone decides.
A program may use at most 64 MiB of HBM per device.

v0:
```python
import jax
import jax.numpy as jnp
from jax import lax
from jax.sharding import PartitionSpec as P

ITERS = 4


interval_delta = 2.0
cooling = 3.0
kind_weights = (1.0, 0.5, 0.25)
kind_counts = (6.0, 12.0, 8.0)


def padded_2(cells, sides, width):
    for axis, dim in sides:
        count = lax.axis_size(axis)
        ends = count - 1
        head = lax.slice_in_dim(cells, 0, width, axis=dim)
        tail = lax.slice_in_dim(cells, cells.shape[dim] - width, cells.shape[dim], axis=dim)
        cells = jnp.concatenate(
            [
                lax.ppermute(tail, axis, [(i, (i + 1) % count) for i in range(ends)]),
                cells,
                lax.ppermute(head, axis, [((i + 1) % count, i) for i in range(ends)]),
            ],
            axis=dim,
        )
    return cells


def split_axis(values, axis):
    length = values.shape[axis] - 2
    center = lax.slice_in_dim(values, 1, length + 1, axis=axis)
    beside = lax.slice_in_dim(values, 0, length, axis=axis) + lax.slice_in_dim(
        values, 2, length + 2, axis=axis
    )
    return (center, beside)


def neighbor_sums(padded):
    leading_extent = padded.ndim - 3
    pieces = [(padded, 0)]
    for shift_vector in range(3):
        next_pieces = []
        for values, neighbors in pieces:
            center, beside = split_axis(values, leading_extent + shift_vector)
            next_pieces.append((center, neighbors))
            next_pieces.append((beside, neighbors + 1))
        pieces = next_pieces
    totals = [None, None, None]
    for values, neighbors in pieces:
        if neighbors > 0:
            if totals[neighbors - 1] is None:
                totals[neighbors - 1] = values
            else:
                totals[neighbors - 1] = totals[neighbors - 1] + values
    return totals


def coupling(padded, padded_flux, cond):
    field_sums = neighbor_sums(padded)
    accumulated_flux = neighbor_sums(padded_flux)
    computed_output = kind_weights[0] * (cond * field_sums[0] + accumulated_flux[0])
    computed_output = computed_output + kind_weights[1] * (
        cond * field_sums[1] + accumulated_flux[1]
    )
    computed_output = computed_output + kind_weights[2] * (
        cond * field_sums[2] + accumulated_flux[2]
    )
    return computed_output


def body(
    opening_warmth_field,
    cellwise_warming_source,
    substance_category_per_voxel,
    thermal_coefficient_table,
    boundary_cooling_flags,
):
    classes = thermal_coefficient_table.shape[0]
    picks = (
        substance_category_per_voxel[None]
        == jnp.arange(classes, dtype=jnp.int32)[:, None, None, None]
    )
    cond = jnp.sum(jnp.where(picks, thermal_coefficient_table[:, None, None, None], 0.0), axis=0)
    padded_cond = padded_2(cond, (("gx", 0), ("gy", 1), ("gz", 2)), 1)
    cond_sums = neighbor_sums(padded_cond)
    spread = kind_weights[0] * (kind_counts[0] * cond + cond_sums[0])
    spread = spread + kind_weights[1] * (kind_counts[1] * cond + cond_sums[1])
    spread = spread + kind_weights[2] * (kind_counts[2] * cond + cond_sums[2])
    diagonal = (
        1.0
        + interval_delta * cooling * boundary_cooling_flags.astype(jnp.float32)
        + 0.5 * interval_delta * spread
    )

    def apply_stencil_matrix(field):
        stacked = jnp.stack([field, cond * field])
        padded_both = padded_2(stacked, (("gx", 1), ("gy", 2), ("gz", 3)), 1)
        padded = padded_both[0]
        padded_flux = padded_both[1]
        return diagonal * field - 0.5 * interval_delta * coupling(padded, padded_flux, cond)

    def two_products(remaining_mismatch, image):
        return lax.psum(
            (jnp.sum(remaining_mismatch * remaining_mismatch), jnp.sum(remaining_mismatch * image)),
            ("gx", "gy", "gz"),
        )

    closing_warmth_field = opening_warmth_field
    remaining_mismatch = opening_warmth_field
    forcing_term = closing_warmth_field + interval_delta * cellwise_warming_source
    remaining_mismatch = forcing_term - apply_stencil_matrix(closing_warmth_field)
    image = apply_stencil_matrix(remaining_mismatch)
    norm_now, product = two_products(remaining_mismatch, image)
    descent_alpha = norm_now / product
    search_heading = remaining_mismatch
    along = image
    for step in range(ITERS):
        closing_warmth_field = closing_warmth_field + descent_alpha * search_heading
        remaining_mismatch = remaining_mismatch - descent_alpha * along
        if step + 1 < ITERS:
            image = apply_stencil_matrix(remaining_mismatch)
            following_norm, product = two_products(remaining_mismatch, image)
            ratio = following_norm / norm_now
            descent_alpha = following_norm / (product - ratio * following_norm / descent_alpha)
            search_heading = remaining_mismatch + ratio * search_heading
            along = image + ratio * along
            norm_now = following_norm
    return (closing_warmth_field, remaining_mismatch)


def solution(mesh):
    in_specs = (
        P("gx", "gy", "gz"),
        P("gx", "gy", "gz"),
        P("gx", "gy", "gz"),
        P(),
        P("gx", "gy", "gz"),
    )
    out_specs = (P("gx", "gy", "gz"), P("gx", "gy", "gz"))
    return jax.shard_map(body, mesh=mesh, in_specs=in_specs, out_specs=out_specs, check_vma=False)
```

profile of v0, /device:TPU:0, one launch (start us, length us, event | category | flops | bytes accessed | tf_op | source)
XLA Modules:
  0.0 341.2 jit_solution(16953283033864008178)
XLA Ops:
  14.0 4.2 %collective-permute-done.3 = f32[10,1,128]{2,1,0:T(1,128)S(1)} collective-permute-done((f32[10,1,128]{2,1,0:T(1,128)S(1)}, f32[10,1,128]{2,1,0:T(1,128)S(1)}, u32[]{:S(2)}, u32[]{:S(2)}) %collective-permute-start.3) | collective-permute-done | bytes 5152 | tf_op jit(solution)/shard_map/ppermute | solution.py:25
  33.2 4.2 %collective-permute-done.9 = f32[2,10,1,128]{3,2,1,0:T(1,128)S(1)} collective-permute-done((f32[2,10,1,128]{3,2,1,0:T(1,128)S(1)}, f32[2,10,1,128]{3,2,1,0:T(1,128)S(1)}, u32[]{:S(2)}, u32[]{:S(2)}) %collective-permute-start.9) | collective-permute-done | bytes 10272 | tf_op jit(solution)/shard_map/ppermute | solution.py:25
  37.6 4.5 %collective-permute-start.10 = (f32[2,10,18,1]{3,2,1,0:T(8,128)S(1)}, f32[2,10,18,1]{3,2,1,0:T(8,128)S(1)}, u32[]{:S(2)}, u32[]{:S(2)}) collective-permute-start(f32[2,10,18,1]{3,2,1,0:T(8,128)S(1)} %get-tuple-element.60), channel_id=1, source_target_pairs={{0,1},{1,2},{2,3},{4,5},{5,6},{6,7},{8,9},{9,10},{10,11},{12,13},{... | collective-permute-start | bytes 4328 | tf_op jit(solution)/shard_map/ppermute | solution.py:23
  43.4 4.9 %collective-permute-done.10 = f32[2,10,18,1]{3,2,1,0:T(8,128)S(1)} collective-permute-done((f32[2,10,18,1]{3,2,1,0:T(8,128)S(1)}, f32[2,10,18,1]{3,2,1,0:T(8,128)S(1)}, u32[]{:S(2)}, u32[]{:S(2)}) %collective-permute-start.10) | collective-permute-done | bytes 1472 | tf_op jit(solution)/shard_map/ppermute | solution.py:23
  48.3 4.3 %collective-permute-done.11 = f32[2,10,18,1]{3,2,1,0:T(8,128)S(1)} collective-permute-done((f32[2,10,18,1]{3,2,1,0:T(8,128)S(1)}, f32[2,10,18,1]{3,2,1,0:T(8,128)S(1)}, u32[]{:S(2)}, u32[]{:S(2)}) %collective-permute-start.11) | collective-permute-done | bytes 1472 | tf_op jit(solution)/shard_map/ppermute | solution.py:25
  62.7 4.2 %collective-permute-done.15 = f32[2,10,1,128]{3,2,1,0:T(1,128)S(1)} collective-permute-done((f32[2,10,1,128]{3,2,1,0:T(1,128)S(1)}, f32[2,10,1,128]{3,2,1,0:T(1,128)S(1)}, u32[]{:S(2)}, u32[]{:S(2)}) %collective-permute-start.15) | collective-permute-done | bytes 10272 | tf_op jit(solution)/shard_map/ppermute | solution.py:25
  71.8 4.6 %collective-permute-done.16 = f32[2,10,18,1]{3,2,1,0:T(8,128)S(1)} collective-permute-done((f32[2,10,18,1]{3,2,1,0:T(8,128)S(1)}, f32[2,10,18,1]{3,2,1,0:T(8,128)S(1)}, u32[]{:S(2)}, u32[]{:S(2)}) %collective-permute-start.16) | collective-permute-done | bytes 1472 | tf_op jit(solution)/shard_map/ppermute | solution.py:23
  76.5 4.1 %collective-permute-done.17 = f32[2,10,18,1]{3,2,1,0:T(8,128)S(1)} collective-permute-done((f32[2,10,18,1]{3,2,1,0:T(8,128)S(1)}, f32[2,10,18,1]{3,2,1,0:T(8,128)S(1)}, u32[]{:S(2)}, u32[]{:S(2)}) %collective-permute-start.17) | collective-permute-done | bytes 1472 | tf_op jit(solution)/shard_map/ppermute | solution.py:25
  82.0 39.5 %all-reduce.3 = (f32[]{:T(128)}, f32[]{:T(128)}) all-reduce(f32[]{:T(128)} %get-tuple-element.9, f32[]{:T(128)} %get-tuple-element.8), channel_id=1, replica_groups=mesh['gx'=4,'gy'=2,'gz'=4] {'gx','gy','gz'}, use_global_device_ids=true, to_apply=%region_2.3 | all-reduce | flops 2 | bytes 16 | tf_op jit(solution)/shard_map/psum | solution.py:106
  125.5 4.3 %collective-permute-done.19 = f32[2,1,16,128]{3,2,1,0:T(8,128)S(1)} collective-permute-done((f32[2,1,16,128]{3,2,1,0:T(8,128)S(1)}, f32[2,1,16,128]{3,2,1,0:T(8,128)S(1)}, u32[]{:S(2)}, u32[]{:S(2)}) %collective-permute-start.19) | collective-permute-done | bytes 16416 | tf_op jit(solution)/shard_map/ppermute | solution.py:25
  133.4 4.2 %collective-permute-done.21 = f32[2,10,1,128]{3,2,1,0:T(1,128)S(1)} collective-permute-done((f32[2,10,1,128]{3,2,1,0:T(1,128)S(1)}, f32[2,10,1,128]{3,2,1,0:T(1,128)S(1)}, u32[]{:S(2)}, u32[]{:S(2)}) %collective-permute-start.21) | collective-permute-done | bytes 10272 | tf_op jit(solution)/shard_map/ppermute | solution.py:25
  141.4 4.9 %collective-permute-done.22 = f32[2,10,18,1]{3,2,1,0:T(8,128)S(1)} collective-permute-done((f32[2,10,18,1]{3,2,1,0:T(8,128)S(1)}, f32[2,10,18,1]{3,2,1,0:T(8,128)S(1)}, u32[]{:S(2)}, u32[]{:S(2)}) %collective-permute-start.22) | collective-permute-done | bytes 1472 | tf_op jit(solution)/shard_map/ppermute | solution.py:23
  146.3 4.3 %collective-permute-done.23 = f32[2,10,18,1]{3,2,1,0:T(8,128)S(1)} collective-permute-done((f32[2,10,18,1]{3,2,1,0:T(8,128)S(1)}, f32[2,10,18,1]{3,2,1,0:T(8,128)S(1)}, u32[]{:S(2)}, u32[]{:S(2)}) %collective-permute-start.23) | collective-permute-done | bytes 1472 | tf_op jit(solution)/shard_map/ppermute | solution.py:25
  152.1 38.7 %all-reduce.2 = (f32[]{:T(128)}, f32[]{:T(128)}) all-reduce(f32[]{:T(128)} %get-tuple-element.7, f32[]{:T(128)} %get-tuple-element.6), channel_id=1, replica_groups=mesh['gx'=4,'gy'=2,'gz'=4] {'gx','gy','gz'}, use_global_device_ids=true, to_apply=%region_6.7 | all-reduce | flops 2 | bytes 16 | tf_op jit(solution)/shard_map/psum | solution.py:106
  198.0 4.3 %collective-permute-done.25 = f32[2,1,16,128]{3,2,1,0:T(8,128)S(1)} collective-permute-done((f32[2,1,16,128]{3,2,1,0:T(8,128)S(1)}, f32[2,1,16,128]{3,2,1,0:T(8,128)S(1)}, u32[]{:S(2)}, u32[]{:S(2)}) %collective-permute-start.25) | collective-permute-done | bytes 16416 | tf_op jit(solution)/shard_map/ppermute | solution.py:25
  205.8 4.2 %collective-permute-done.27 = f32[2,10,1,128]{3,2,1,0:T(1,128)S(1)} collective-permute-done((f32[2,10,1,128]{3,2,1,0:T(1,128)S(1)}, f32[2,10,1,128]{3,2,1,0:T(1,128)S(1)}, u32[]{:S(2)}, u32[]{:S(2)}) %collective-permute-start.27) | collective-permute-done | bytes 10272 | tf_op jit(solution)/shard_map/ppermute | solution.py:25
  214.6 4.9 %collective-permute-done.28 = f32[2,10,18,1]{3,2,1,0:T(8,128)S(1)} collective-permute-done((f32[2,10,18,1]{3,2,1,0:T(8,128)S(1)}, f32[2,10,18,1]{3,2,1,0:T(8,128)S(1)}, u32[]{:S(2)}, u32[]{:S(2)}) %collective-permute-start.28) | collective-permute-done | bytes 1472 | tf_op jit(solution)/shard_map/ppermute | solution.py:23
  219.5 4.3 %collective-permute-done.29 = f32[2,10,18,1]{3,2,1,0:T(8,128)S(1)} collective-permute-done((f32[2,10,18,1]{3,2,1,0:T(8,128)S(1)}, f32[2,10,18,1]{3,2,1,0:T(8,128)S(1)}, u32[]{:S(2)}, u32[]{:S(2)}) %collective-permute-start.29) | collective-permute-done | bytes 1472 | tf_op jit(solution)/shard_map/ppermute | solution.py:25
  225.2 38.8 %all-reduce.1 = (f32[]{:T(128)}, f32[]{:T(128)}) all-reduce(f32[]{:T(128)} %get-tuple-element.5, f32[]{:T(128)} %get-tuple-element.4), channel_id=1, replica_groups=mesh['gx'=4,'gy'=2,'gz'=4] {'gx','gy','gz'}, use_global_device_ids=true, to_apply=%region_10.11 | all-reduce | flops 2 | bytes 16 | tf_op jit(solution)/shard_map/psum | solution.py:106
  270.6 4.3 %collective-permute-done.31 = f32[2,1,16,128]{3,2,1,0:T(8,128)S(1)} collective-permute-done((f32[2,1,16,128]{3,2,1,0:T(8,128)S(1)}, f32[2,1,16,128]{3,2,1,0:T(8,128)S(1)}, u32[]{:S(2)}, u32[]{:S(2)}) %collective-permute-start.31) | collective-permute-done | bytes 16416 | tf_op jit(solution)/shard_map/ppermute | solution.py:25
  278.4 4.2 %collective-permute-done.33 = f32[2,10,1,128]{3,2,1,0:T(1,128)S(1)} collective-permute-done((f32[2,10,1,128]{3,2,1,0:T(1,128)S(1)}, f32[2,10,1,128]{3,2,1,0:T(1,128)S(1)}, u32[]{:S(2)}, u32[]{:S(2)}) %collective-permute-start.33) | collective-permute-done | bytes 10272 | tf_op jit(solution)/shard_map/ppermute | solution.py:25
  287.2 4.9 %collective-permute-done.34 = f32[2,10,18,1]{3,2,1,0:T(8,128)S(1)} collective-permute-done((f32[2,10,18,1]{3,2,1,0:T(8,128)S(1)}, f32[2,10,18,1]{3,2,1,0:T(8,128)S(1)}, u32[]{:S(2)}, u32[]{:S(2)}) %collective-permute-start.34) | collective-permute-done | bytes 1472 | tf_op jit(solution)/shard_map/ppermute | solution.py:23
  292.2 4.3 %collective-permute-done.35 = f32[2,10,18,1]{3,2,1,0:T(8,128)S(1)} collective-permute-done((f32[2,10,18,1]{3,2,1,0:T(8,128)S(1)}, f32[2,10,18,1]{3,2,1,0:T(8,128)S(1)}, u32[]{:S(2)}, u32[]{:S(2)}) %collective-permute-start.35) | collective-permute-done | bytes 1472 | tf_op jit(solution)/shard_map/ppermute | solution.py:25
  297.9 38.7 %all-reduce = (f32[]{:T(128)}, f32[]{:T(128)}) all-reduce(f32[]{:T(128)} %get-tuple-element.3, f32[]{:T(128)} %get-tuple-element.2), channel_id=1, replica_groups=mesh['gx'=4,'gy'=2,'gz'=4] {'gx','gy','gz'}, use_global_device_ids=true, to_apply=%region_14.15 | all-reduce | flops 2 | bytes 16 | tf_op jit(solution)/shard_map/psum | solution.py:106
  (125 shorter events, 82.3 us)
Async XLA Ops:
  4.1 5.2 %collective-permute-start.1 = (f32[1,16,128]{2,1,0:T(8,128)S(1)}, f32[1,16,128]{2,1,0:T(8,128)S(1)}, u32[]{:S(2)}, u32[]{:S(2)}) collective-permute-start(f32[1,16,128]{2,1,0:T(8,128)S(1)} %get-tuple-element.89), channel_id=1, source_target_pairs={{8,0},{16,8},{24,16},{9,1},{17,9},{25,17},{10,2},{18,10},{26,18},{... | collective-permute-start | bytes 24584 | tf_op jit(solution)/shard_map/ppermute | solution.py:25
  9.3 4.8 %collective-permute-start.2 = (f32[10,1,128]{2,1,0:T(1,128)S(1)}, f32[10,1,128]{2,1,0:T(1,128)S(1)}, u32[]{:S(2)}, u32[]{:S(2)}) collective-permute-start(f32[10,1,128]{2,1,0:T(1,128)S(1)} %get-tuple-element.84), channel_id=1, source_target_pairs={{0,4},{1,5},{2,6},{3,7},{8,12},{9,13},{10,14},{11,15},{16,20},{17,... | collective-permute-start | bytes 15368 | tf_op jit(solution)/shard_map/ppermute | solution.py:23
  12.7 5.5 %collective-permute-start.3 = (f32[10,1,128]{2,1,0:T(1,128)S(1)}, f32[10,1,128]{2,1,0:T(1,128)S(1)}, u32[]{:S(2)}, u32[]{:S(2)}) collective-permute-start(f32[10,1,128]{2,1,0:T(1,128)S(1)} %get-tuple-element.85), channel_id=1, source_target_pairs={{4,0},{5,1},{6,2},{7,3},{12,8},{13,9},{14,10},{15,11},{20,16},{21,... | collective-permute-start | bytes 15368 | tf_op jit(solution)/shard_map/ppermute | solution.py:25
  18.3 8.7 %collective-permute-start.4 = (f32[10,18,1]{2,1,0:T(8,128)S(1)}, f32[10,18,1]{2,1,0:T(8,128)S(1)}, u32[]{:S(2)}, u32[]{:S(2)}) collective-permute-start(f32[10,18,1]{2,1,0:T(8,128)S(1)} %get-tuple-element.82), channel_id=1, source_target_pairs={{0,1},{1,2},{2,3},{4,5},{5,6},{6,7},{8,9},{9,10},{10,11},{12,13},{... | collective-permute-start | bytes 2168 | tf_op jit(solution)/shard_map/ppermute | solution.py:23
  21.8 7.8 %collective-permute-start.5 = (f32[10,18,1]{2,1,0:T(8,128)S(1)}, f32[10,18,1]{2,1,0:T(8,128)S(1)}, u32[]{:S(2)}, u32[]{:S(2)}) collective-permute-start(f32[10,18,1]{2,1,0:T(8,128)S(1)} %get-tuple-element.83), channel_id=1, source_target_pairs={{1,0},{2,1},{3,2},{5,4},{6,5},{7,6},{9,8},{10,9},{11,10},{13,12},{... | collective-permute-start | bytes 2168 | tf_op jit(solution)/shard_map/ppermute | solution.py:25
  23.1 6.7 %collective-permute-start.6 = (f32[2,1,16,128]{3,2,1,0:T(8,128)S(1)}, f32[2,1,16,128]{3,2,1,0:T(8,128)S(1)}, u32[]{:S(2)}, u32[]{:S(2)}) collective-permute-start(f32[2,1,16,128]{3,2,1,0:T(8,128)S(1)} %get-tuple-element.80), channel_id=1, source_target_pairs={{0,8},{8,16},{16,24},{1,9},{9,17},{17,25},{2,10},{10,18},{18,26},{... | collective-permute-start | bytes 49160 | tf_op jit(solution)/shard_map/ppermute | solution.py:23
  31.8 5.6 %collective-permute-start.9 = (f32[2,10,1,128]{3,2,1,0:T(1,128)S(1)}, f32[2,10,1,128]{3,2,1,0:T(1,128)S(1)}, u32[]{:S(2)}, u32[]{:S(2)}) collective-permute-start(f32[2,10,1,128]{3,2,1,0:T(1,128)S(1)} %get-tuple-element.71), channel_id=1, source_target_pairs={{4,0},{5,1},{6,2},{7,3},{12,8},{13,9},{14,10},{15,11},{20,16},{21,... | collective-permute-start | bytes 30728 | tf_op jit(solution)/shard_map/ppermute | solution.py:25
  37.6 10.7 %collective-permute-start.10 = (f32[2,10,18,1]{3,2,1,0:T(8,128)S(1)}, f32[2,10,18,1]{3,2,1,0:T(8,128)S(1)}, u32[]{:S(2)}, u32[]{:S(2)}) collective-permute-start(f32[2,10,18,1]{3,2,1,0:T(8,128)S(1)} %get-tuple-element.60), channel_id=1, source_target_pairs={{0,1},{1,2},{2,3},{4,5},{5,6},{6,7},{8,9},{9,10},{10,11},{12,13},{... | collective-permute-start | bytes 4328 | tf_op jit(solution)/shard_map/ppermute | solution.py:23
  42.1 10.5 %collective-permute-start.11 = (f32[2,10,18,1]{3,2,1,0:T(8,128)S(1)}, f32[2,10,18,1]{3,2,1,0:T(8,128)S(1)}, u32[]{:S(2)}, u32[]{:S(2)}) collective-permute-start(f32[2,10,18,1]{3,2,1,0:T(8,128)S(1)} %get-tuple-element.61), channel_id=1, source_target_pairs={{1,0},{2,1},{3,2},{5,4},{6,5},{7,6},{9,8},{10,9},{11,10},{13,12},{... | collective-permute-start | bytes 4328 | tf_op jit(solution)/shard_map/ppermute | solution.py:25
  61.3 5.6 %collective-permute-start.15 = (f32[2,10,1,128]{3,2,1,0:T(1,128)S(1)}, f32[2,10,1,128]{3,2,1,0:T(1,128)S(1)}, u32[]{:S(2)}, u32[]{:S(2)}) collective-permute-start(f32[2,10,1,128]{3,2,1,0:T(1,128)S(1)} %get-tuple-element.69), channel_id=1, source_target_pairs={{4,0},{5,1},{6,2},{7,3},{12,8},{13,9},{14,10},{15,11},{20,16},{21,... | collective-permute-start | bytes 30728 | tf_op jit(solution)/shard_map/ppermute | solution.py:25
  67.1 9.4 %collective-permute-start.16 = (f32[2,10,18,1]{3,2,1,0:T(8,128)S(1)}, f32[2,10,18,1]{3,2,1,0:T(8,128)S(1)}, u32[]{:S(2)}, u32[]{:S(2)}) collective-permute-start(f32[2,10,18,1]{3,2,1,0:T(8,128)S(1)} %get-tuple-element.58), channel_id=1, source_target_pairs={{0,1},{1,2},{2,3},{4,5},{5,6},{6,7},{8,9},{9,10},{10,11},{12,13},{... | collective-permute-start | bytes 4328 | tf_op jit(solution)/shard_map/ppermute | solution.py:23
  70.5 10.0 %collective-permute-start.17 = (f32[2,10,18,1]{3,2,1,0:T(8,128)S(1)}, f32[2,10,18,1]{3,2,1,0:T(8,128)S(1)}, u32[]{:S(2)}, u32[]{:S(2)}) collective-permute-start(f32[2,10,18,1]{3,2,1,0:T(8,128)S(1)} %get-tuple-element.59), channel_id=1, source_target_pairs={{1,0},{2,1},{3,2},{5,4},{6,5},{7,6},{9,8},{10,9},{11,10},{13,12},{... | collective-permute-start | bytes 4328 | tf_op jit(solution)/shard_map/ppermute | solution.py:25
  124.2 5.6 %collective-permute-start.19 = (f32[2,1,16,128]{3,2,1,0:T(8,128)S(1)}, f32[2,1,16,128]{3,2,1,0:T(8,128)S(1)}, u32[]{:S(2)}, u32[]{:S(2)}) collective-permute-start(f32[2,1,16,128]{3,2,1,0:T(8,128)S(1)} %get-tuple-element.77), channel_id=1, source_target_pairs={{8,0},{16,8},{24,16},{9,1},{17,9},{25,17},{10,2},{18,10},{26,18},{... | collective-permute-start | bytes 49160 | tf_op jit(solution)/shard_map/ppermute | solution.py:25
  132.0 5.6 %collective-permute-start.21 = (f32[2,10,1,128]{3,2,1,0:T(1,128)S(1)}, f32[2,10,1,128]{3,2,1,0:T(1,128)S(1)}, u32[]{:S(2)}, u32[]{:S(2)}) collective-permute-start(f32[2,10,1,128]{3,2,1,0:T(1,128)S(1)} %get-tuple-element.67), channel_id=1, source_target_pairs={{4,0},{5,1},{6,2},{7,3},{12,8},{13,9},{14,10},{15,11},{20,16},{21,... | collective-permute-start | bytes 30728 | tf_op jit(solution)/shard_map/ppermute | solution.py:25
  137.8 8.6 %collective-permute-start.22 = (f32[2,10,18,1]{3,2,1,0:T(8,128)S(1)}, f32[2,10,18,1]{3,2,1,0:T(8,128)S(1)}, u32[]{:S(2)}, u32[]{:S(2)}) collective-permute-start(f32[2,10,18,1]{3,2,1,0:T(8,128)S(1)} %get-tuple-element.56), channel_id=1, source_target_pairs={{0,1},{1,2},{2,3},{4,5},{5,6},{6,7},{8,9},{9,10},{10,11},{12,13},{... | collective-permute-start | bytes 4328 | tf_op jit(solution)/shard_map/ppermute | solution.py:23
  140.1 10.5 %collective-permute-start.23 = (f32[2,10,18,1]{3,2,1,0:T(8,128)S(1)}, f32[2,10,18,1]{3,2,1,0:T(8,128)S(1)}, u32[]{:S(2)}, u32[]{:S(2)}) collective-permute-start(f32[2,10,18,1]{3,2,1,0:T(8,128)S(1)} %get-tuple-element.57), channel_id=1, source_target_pairs={{1,0},{2,1},{3,2},{5,4},{6,5},{7,6},{9,8},{10,9},{11,10},{13,12},{... | collective-permute-start | bytes 4328 | tf_op jit(solution)/shard_map/ppermute | solution.py:25
  196.6 5.6 %collective-permute-start.25 = (f32[2,1,16,128]{3,2,1,0:T(8,128)S(1)}, f32[2,1,16,128]{3,2,1,0:T(8,128)S(1)}, u32[]{:S(2)}, u32[]{:S(2)}) collective-permute-start(f32[2,1,16,128]{3,2,1,0:T(8,128)S(1)} %get-tuple-element.75), channel_id=1, source_target_pairs={{8,0},{16,8},{24,16},{9,1},{17,9},{25,17},{10,2},{18,10},{26,18},{... | collective-permute-start | bytes 49160 | tf_op jit(solution)/shard_map/ppermute | solution.py:25
  204.5 5.6 %collective-permute-start.27 = (f32[2,10,1,128]{3,2,1,0:T(1,128)S(1)}, f32[2,10,1,128]{3,2,1,0:T(1,128)S(1)}, u32[]{:S(2)}, u32[]{:S(2)}) collective-permute-start(f32[2,10,1,128]{3,2,1,0:T(1,128)S(1)} %get-tuple-element.65), channel_id=1, source_target_pairs={{4,0},{5,1},{6,2},{7,3},{12,8},{13,9},{14,10},{15,11},{20,16},{21,... | collective-permute-start | bytes 30728 | tf_op jit(solution)/shard_map/ppermute | solution.py:25
  210.2 9.3 %collective-permute-start.28 = (f32[2,10,18,1]{3,2,1,0:T(8,128)S(1)}, f32[2,10,18,1]{3,2,1,0:T(8,128)S(1)}, u32[]{:S(2)}, u32[]{:S(2)}) collective-permute-start(f32[2,10,18,1]{3,2,1,0:T(8,128)S(1)} %get-tuple-element.54), channel_id=1, source_target_pairs={{0,1},{1,2},{2,3},{4,5},{5,6},{6,7},{8,9},{9,10},{10,11},{12,13},{... | collective-permute-start | bytes 4328 | tf_op jit(solution)/shard_map/ppermute | solution.py:23
  213.3 10.5 %collective-permute-start.29 = (f32[2,10,18,1]{3,2,1,0:T(8,128)S(1)}, f32[2,10,18,1]{3,2,1,0:T(8,128)S(1)}, u32[]{:S(2)}, u32[]{:S(2)}) collective-permute-start(f32[2,10,18,1]{3,2,1,0:T(8,128)S(1)} %get-tuple-element.55), channel_id=1, source_target_pairs={{1,0},{2,1},{3,2},{5,4},{6,5},{7,6},{9,8},{10,9},{11,10},{13,12},{... | collective-permute-start | bytes 4328 | tf_op jit(solution)/shard_map/ppermute | solution.py:25
  269.3 5.6 %collective-permute-start.31 = (f32[2,1,16,128]{3,2,1,0:T(8,128)S(1)}, f32[2,1,16,128]{3,2,1,0:T(8,128)S(1)}, u32[]{:S(2)}, u32[]{:S(2)}) collective-permute-start(f32[2,1,16,128]{3,2,1,0:T(8,128)S(1)} %get-tuple-element.73), channel_id=1, source_target_pairs={{8,0},{16,8},{24,16},{9,1},{17,9},{25,17},{10,2},{18,10},{26,18},{... | collective-permute-start | bytes 49160 | tf_op jit(solution)/shard_map/ppermute | solution.py:25
  277.1 5.6 %collective-permute-start.33 = (f32[2,10,1,128]{3,2,1,0:T(1,128)S(1)}, f32[2,10,1,128]{3,2,1,0:T(1,128)S(1)}, u32[]{:S(2)}, u32[]{:S(2)}) collective-permute-start(f32[2,10,1,128]{3,2,1,0:T(1,128)S(1)} %get-tuple-element.63), channel_id=1, source_target_pairs={{4,0},{5,1},{6,2},{7,3},{12,8},{13,9},{14,10},{15,11},{20,16},{21,... | collective-permute-start | bytes 30728 | tf_op jit(solution)/shard_map/ppermute | solution.py:25
  282.8 9.3 %collective-permute-start.34 = (f32[2,10,18,1]{3,2,1,0:T(8,128)S(1)}, f32[2,10,18,1]{3,2,1,0:T(8,128)S(1)}, u32[]{:S(2)}, u32[]{:S(2)}) collective-permute-start(f32[2,10,18,1]{3,2,1,0:T(8,128)S(1)} %get-tuple-element.52), channel_id=1, source_target_pairs={{0,1},{1,2},{2,3},{4,5},{5,6},{6,7},{8,9},{9,10},{10,11},{12,13},{... | collective-permute-start | bytes 4328 | tf_op jit(solution)/shard_map/ppermute | solution.py:23
  285.9 10.5 %collective-permute-start.35 = (f32[2,10,18,1]{3,2,1,0:T(8,128)S(1)}, f32[2,10,18,1]{3,2,1,0:T(8,128)S(1)}, u32[]{:S(2)}, u32[]{:S(2)}) collective-permute-start(f32[2,10,18,1]{3,2,1,0:T(8,128)S(1)} %get-tuple-element.53), channel_id=1, source_target_pairs={{1,0},{2,1},{3,2},{5,4},{6,5},{7,6},{9,8},{10,9},{11,10},{13,12},{... | collective-permute-start | bytes 4328 | tf_op jit(solution)/shard_map/ppermute | solution.py:25
  (15 other events, 53.2 us)
where the time goes:
time: 343 us; the launch traced here: 341 us
  blocking collectives  156 us (45%)
  waiting for transfers between devices  92.3 us (27%)
  starting transfers between devices  67.6 us (20%)
  between operations  15.1 us (4%)
  other arithmetic  8.92 us (3%)
    psum x4, blocking collectives, two_products(): lax.psum((jnp.sum(remaining_mismatch * remaining_mismatch), jnp.sum(remai...  156 us
    ppermute x18, waiting for transfers between devices, padded_2(): lax.ppermute(head, axis, [((i + 1) % count, i) for i in range(ends)])  67.7 us
    ppermute x18, starting transfers between devices, padded_2(): lax.ppermute(tail, axis, [(i, (i + 1) % count) for i in range(ends)])  44.3 us
    ppermute x18, waiting for transfers between devices, padded_2(): lax.ppermute(tail, axis, [(i, (i + 1) % count) for i in range(ends)])  24.7 us
    ppermute x18, starting transfers between devices, padded_2(): lax.ppermute(head, axis, [((i + 1) % count, i) for i in range(ends)])  23.3 us
  transfers between devices with their start and end apart: 36, of which 27 were waited for; matrix products, arithmetic and copies ran while one was open for 0% of the time, Pallas kernels for 0%

commit v1 on v0

v1 whole, which is shorter than its diff:
```python
import functools

import jax
import jax.numpy as jnp
from jax import lax
from jax.experimental import pallas as pl
from jax.experimental.pallas import tpu as pltpu
from jax.sharding import PartitionSpec as P

ITERS = 4
interval_delta = 2.0
cooling = 3.0

MESH = pl.DeviceIdType.MESH
AXES = ("gx", "gy", "gz")
SUB = 8
LANES = 128
FIELDS = 4
WARM, SOURCE, COND, FLAGS, EDGES = range(5)
SLOT = LANES // FIELDS
PAIRS = [(i, j) for i in range(ITERS + 1) for j in range(i, ITERS + 1) if i < ITERS]


def smooth(values, axis):
    size = values.shape[axis]
    once = values + pltpu.roll(values, 1, axis)
    return once + pltpu.roll(once, size - 1, axis)


def smooth_all(before, center, after):
    return smooth(smooth(before + (center + center) + after, 0), 1)


def kernel(
    counts,
    warm_in,
    source_in,
    category_in,
    table_in,
    flags_in,
    warm_out,
    left_out,
    grid,
    basis,
    flux,
    diag,
    table,
    ints,
    edges,
    beside,
    bound_row,
    bound_rows,
    gram_row,
    gram_rows,
    load_sems,
    raw_send,
    raw_recv,
    fwd_send,
    fwd_recv,
    z_send,
    z_recv,
    row_send,
    row_recv,
):
    devices = counts[0] * counts[1] * counts[2]
    nx, ny, nz = warm_out.shape
    depth = ITERS + 1
    wide, tall, long = grid.shape[1:]
    here = [lax.axis_index(a) for a in AXES]
    me = (here[0] * counts[1] + here[1]) * counts[2] + here[2]

    def at(linear):
        return {
            "gx": linear // (counts[1] * counts[2]),
            "gy": (linear // counts[2]) % counts[1],
            "gz": linear % counts[2],
        }

    main = (slice(depth, depth + nx), slice(0, ny), slice(0, nz))
    loads = [
        pltpu.make_async_copy(category_in, ints.at[0], load_sems.at[0]),
        pltpu.make_async_copy(flags_in, ints.at[1], load_sems.at[1]),
        pltpu.make_async_copy(
            warm_in, grid.at[WARM, pl.ds(depth, nx), pl.ds(0, ny), pl.ds(0, nz)], load_sems.at[2]
        ),
        pltpu.make_async_copy(
            source_in, grid.at[SOURCE, pl.ds(depth, nx), pl.ds(0, ny), pl.ds(0, nz)], load_sems.at[3]
        ),
    ]
    for load in loads[:2]:
        load.start()

    for f in range(FIELDS + 1):
        grid[f, 0:depth, :, 0:nz] = jnp.zeros((depth, tall, nz), jnp.float32)
        grid[f, depth + nx :, :, 0:nz] = jnp.zeros((depth, tall, nz), jnp.float32)
        grid[f, depth : depth + nx, ny:, 0:nz] = jnp.zeros((nx, tall - ny, nz), jnp.float32)
    beside[...] = jnp.zeros(beside.shape, jnp.float32)
    for load in loads[2:]:
        load.start()

    barrier = pltpu.get_barrier_semaphore()

    @pl.loop(1, devices)
    def _(step):
        pl.semaphore_signal(
            barrier, inc=1, device_id=at((me + step) % devices), device_id_type=MESH
        )

    for load in loads:
        load.wait()

    lookup = jnp.broadcast_to(table_in[...], (ny, LANES))
    lane = lax.broadcasted_iota(jnp.int32, (ny, LANES), 1)
    top = jnp.zeros((ny, LANES), jnp.float32)
    total = jnp.zeros((ny, LANES), jnp.float32)
    most = jnp.zeros((ny, LANES), jnp.float32)
    least = jnp.ones((ny, LANES), jnp.float32)
    for i in range(nx):
        cond = jnp.take_along_axis(lookup, ints[0, i], axis=1)
        flag = ints[1, i].astype(jnp.float32)
        grid[COND, depth + i, 0:ny, 0:nz] = cond
        grid[FLAGS, depth + i, 0:ny, 0:nz] = flag
        pieces = [
            grid[WARM, depth + i, 0:ny, 0:nz],
            grid[SOURCE, depth + i, 0:ny, 0:nz],
            cond,
            flag,
        ]
        packed = None
        for f, piece in enumerate(pieces):
            turned = pltpu.roll(piece, (f * SLOT + SLOT // 2) % LANES, 1)
            packed = turned if packed is None else jnp.where(lane // SLOT == f, turned, packed)
        edges[i] = packed
        top = jnp.maximum(top, cond)
        total = total + cond
        most = jnp.maximum(most, flag)
        least = jnp.minimum(least, flag)
    shrink = lambda op, v: op(op(v, axis=0, keepdims=True), axis=1, keepdims=True)
    mean = shrink(jnp.sum, total) * (1.0 / (nx * ny * nz))
    high = 1.0 + interval_delta * cooling * shrink(jnp.max, most)
    high = high + 8.0 * interval_delta * (shrink(jnp.max, top) + mean)
    low = 1.0 + interval_delta * cooling * shrink(jnp.min, least)
    row_lane = lax.broadcasted_iota(jnp.int32, (1, LANES), 1)
    row = jnp.where(row_lane == 0, high, -low)
    bound_row[...] = row
    bound_rows[me] = row

    pl.semaphore_wait(barrier, devices - 1)

    def remote(src, dst, send, recv, offset):
        return pltpu.make_async_remote_copy(
            src_ref=src,
            dst_ref=dst,
            send_sem=send,
            recv_sem=recv,
            device_id={a: here[k] + offset[k] for k, a in enumerate(AXES)},
            device_id_type=MESH,
        )

    def exists(offset):
        good = None
        for k in range(3):
            if offset[k] > 0:
                one = here[k] < counts[k] - 1
            elif offset[k] < 0:
                one = here[k] > 0
            else:
                continue
            good = one if good is None else jnp.logical_and(good, one)
        return good

    z_copies = []
    for k, dz in enumerate((1, -1)):
        copy = remote(edges, beside.at[k], z_send.at[k], z_recv.at[k], (0, 0, dz))
        z_copies.append((copy, dz))
        pl.when(exists((0, 0, dz)))(copy.start)

    def spread(row_ref, rows_ref, k):
        @pl.loop(1, devices)
        def _(step):
            pltpu.make_async_remote_copy(
                src_ref=row_ref,
                dst_ref=rows_ref.at[me],
                send_sem=row_send.at[k],
                recv_sem=row_recv.at[k],
                device_id=at((me + step) % devices),
                device_id_type=MESH,
            ).start()

    def spread_wait(rows_ref, k):
        whole = pltpu.make_async_remote_copy(
            src_ref=rows_ref.at[pl.ds(0, devices - 1)],
            dst_ref=rows_ref.at[pl.ds(0, devices - 1)],
            send_sem=row_send.at[k],
            recv_sem=row_recv.at[k],
            device_id=at((me + 1) % devices),
            device_id_type=MESH,
        )
        whole.wait_send()
        whole.wait_recv()

    if devices > 1:
        spread(bound_row, bound_rows, 0)

    def ranges(offset):
        dx, dy = offset
        if dx == 0:
            xs, xd, xn = depth, depth, nx
        elif dx > 0:
            xs, xd, xn = nx, 0, depth
        else:
            xs, xd, xn = depth, depth + nx, depth
        if dy == 0:
            ys, yd, yn = 0, 0, ny
        elif dy > 0:
            ys, yd, yn = ny - SUB, ny + SUB, SUB
        else:
            ys, yd, yn = 0, ny, SUB
        z = pl.ds(0, nz)
        return (pl.ds(xs, xn), pl.ds(ys, yn), z), (pl.ds(xd, xn), pl.ds(yd, yn), z)

    offsets = [(0, 1), (0, -1), (1, 1), (-1, -1), (1, -1), (-1, 1), (1, 0), (-1, 0)]

    def around(fields, sends, recvs):
        copies = []
        for k, offset in enumerate(offsets):
            src, dst = ranges(offset)
            copies.append(
                (
                    remote(
                        grid.at[(fields,) + src],
                        grid.at[(fields,) + dst],
                        sends.at[k],
                        recvs.at[k],
                        offset + (0,),
                    ),
                    offset,
                )
            )
        return copies

    raw = around(pl.ds(0, FIELDS), raw_send, raw_recv)
    fwd = around(pl.ds(EDGES, 1), fwd_send, fwd_recv)
    for copy, (dx, dy) in raw:
        pl.when(exists((dx, dy, 0)))(copy.start)

    for copy, dz in z_copies:
        pl.when(exists((0, 0, -dz)))(copy.wait_recv)
    low_half = lane % SLOT < SLOT // 2
    for i in range(nx):
        grid[EDGES, depth + i, 0:ny, 0:nz] = jnp.where(low_half, beside[0, i], beside[1, i])
    for copy, (dx, dy) in fwd:
        pl.when(exists((dx, dy, 0)))(copy.start)

    for copy, (dx, dy) in raw:
        pl.when(exists((-dx, -dy, 0)))(copy.wait_recv)
    for copy, (dx, dy) in fwd:
        pl.when(exists((-dx, -dy, 0)))(copy.wait_recv)

    for i in range(wide):
        packed = grid[EDGES, i, :, 0:nz]
        for f in range(FIELDS):
            grid[f, i, :, nz:] = pltpu.roll(packed, (-f * SLOT - SLOT // 2) % LANES, 1)
        flux[0, i] = grid[COND, i] * grid[WARM, i]

    if devices > 1:
        spread_wait(bound_rows, 0)
    bounds = jnp.max(bound_rows[...], axis=0)
    pick = lambda v, i: jnp.sum(jnp.where(row_lane == i, v, 0.0), axis=1, keepdims=True)
    high, low = pick(bounds, 0), -pick(bounds, 1)
    middle = 0.5 * (high + low)
    half = 0.5 * (high - low)
    scale = 1.0 / half

    def valid(index, size, k):
        inner = index < size
        right = jnp.logical_and(index < size + (SUB if k == 1 else LANES // 2), here[k] < counts[k] - 1)
        left = jnp.logical_and(index >= size + (SUB if k == 1 else LANES // 2), here[k] > 0)
        return jnp.logical_or(inner, jnp.logical_or(right, left))

    y_index = lax.broadcasted_iota(jnp.int32, (tall, long), 0)
    z_index = lax.broadcasted_iota(jnp.int32, (tall, long), 1)
    inside = jnp.where(
        jnp.logical_and(valid(y_index, ny, 1), valid(z_index, nz, 2)), 0.125 * interval_delta, 0.0
    )
    x_left = jnp.where(here[0] > 0, 1.0, 0.0)
    x_right = jnp.where(here[0] < counts[0] - 1, 1.0, 0.0)

    def mask(i):
        if i < depth:
            return inside * x_left
        if i >= depth + nx:
            return inside * x_right
        return inside

    quarter = 0.125 * interval_delta

    for i in range(1, wide - 1):
        cond = grid[COND, i]
        ring = smooth_all(grid[COND, i - 1], cond, grid[COND, i + 1])
        d = 1.0 + interval_delta * cooling * grid[FLAGS, i] + 8.0 * interval_delta * cond + quarter * ring
        diag[i] = d
        warm = grid[WARM, i]
        own = smooth_all(grid[WARM, i - 1], warm, grid[WARM, i + 1])
        push = smooth_all(flux[0, i - 1], flux[0, i], flux[0, i + 1])
        image = d * warm - (quarter * cond * own + mask(i) * push)
        left = warm + interval_delta * grid[SOURCE, i] - image
        basis[0, i] = left
        flux[1, i] = cond * left

    for k in range(ITERS):
        now, later = (k + 1) % 2, k % 2
        for i in range(2 + k, wide - 2 - k):
            cond = grid[COND, i]
            mid = basis[k, i]
            own = smooth_all(basis[k, i - 1], mid, basis[k, i + 1])
            push = smooth_all(flux[now, i - 1], flux[now, i], flux[now, i + 1])
            image = (diag[i] - middle) * mid - (quarter * cond * own + mask(i) * push)
            if k == 0:
                fresh = scale * image
            else:
                fresh = (2.0 * scale) * image - basis[k - 1, i]
            basis[k + 1, i] = fresh
            if k + 1 < ITERS:
                flux[later, i] = cond * fresh

    sums = [None] * len(PAIRS)
    for i in range(depth, depth + nx):
        rows = [basis[k, i, 0:ny, 0:nz] for k in range(ITERS + 1)]
        for n, (a, b) in enumerate(PAIRS):
            term = rows[a] * rows[b]
            sums[n] = term if sums[n] is None else sums[n] + term
    diagonal = lax.broadcasted_iota(jnp.int32, (SUB, LANES), 0)
    across = lax.broadcasted_iota(jnp.int32, (SUB, LANES), 1)
    row = jnp.zeros((SUB, LANES), jnp.float32)
    for start in range(0, len(PAIRS), SUB):
        tile = jnp.zeros((SUB, LANES), jnp.float32)
        for n in range(start, min(start + SUB, len(PAIRS))):
            tile = jnp.where(diagonal == n - start, jnp.sum(sums[n], axis=0, keepdims=True), tile)
        column = jnp.sum(tile, axis=1, keepdims=True)
        row = row + jnp.where(across == diagonal + start, column, 0.0)
    row = jnp.sum(row, axis=0, keepdims=True)
    gram_row[...] = row
    gram_rows[me] = row
    if devices > 1:
        spread(gram_row, gram_rows, 1)
        spread_wait(gram_rows, 1)
    row = jnp.sum(gram_rows[...], axis=0)
    gram = {}
    for n, (a, b) in enumerate(PAIRS):
        gram[a, b] = gram[b, a] = pick(row, n)

    def apply(p):
        q = [middle * a for a in p] + [None]
        q[len(p)] = jnp.zeros_like(half)
        for i, a in enumerate(p):
            if i == 0:
                q[1] = q[1] + half * a
            else:
                q[i + 1] = q[i + 1] + (0.5 * half) * a
                q[i - 1] = q[i - 1] + (0.5 * half) * a
        return q

    def product(p, q):
        value = None
        for i, a in enumerate(p):
            inner = None
            for j, b in enumerate(q):
                term = gram[i, j] * b
                inner = term if inner is None else inner + term
            inner = a * inner
            value = inner if value is None else value + inner
        return value

    left = [jnp.ones_like(half)]
    heading = list(left)
    moved = []
    norm = product(left, left)
    for step in range(ITERS):
        image = apply(heading)
        alpha = norm / product(heading, image)
        moved = [a + alpha * b for a, b in zip(moved, heading)] + [
            alpha * b for b in heading[len(moved) :]
        ]
        left = [a - alpha * b for a, b in zip(left, image)] + [
            -alpha * b for b in image[len(left) :]
        ]
        if step + 1 < ITERS:
            following = product(left, left)
            ratio = following / norm
            heading = [a + ratio * b for a, b in zip(left, heading)] + left[len(heading) :]
            norm = following

    for i in range(nx):
        warm = grid[WARM, depth + i, 0:ny, 0:nz]
        end = jnp.zeros_like(warm)
        for k in range(ITERS + 1):
            value = basis[k, depth + i, 0:ny, 0:nz]
            if k < ITERS:
                warm = warm + moved[k] * value
            end = end + left[k] * value
        warm_out[i] = warm
        left_out[i] = end

    for copy, dz in z_copies:
        pl.when(exists((0, 0, dz)))(copy.wait_send)
    for copy, (dx, dy) in raw + fwd:
        pl.when(exists((dx, dy, 0)))(copy.wait_send)


def body(counts, warm, source, category, table, flags):
    nx, ny, nz = warm.shape
    depth = ITERS + 1
    devices = counts[0] * counts[1] * counts[2]
    wide, tall, long = nx + 2 * depth, ny + 2 * SUB, nz + LANES
    table = jnp.pad(table, (0, LANES - table.shape[0]))[None]
    any_spec = pl.BlockSpec(memory_space=pl.ANY)
    vmem = pl.BlockSpec(memory_space=pltpu.VMEM)
    shape = jax.ShapeDtypeStruct(warm.shape, jnp.float32)
    f32 = jnp.float32
    return pl.pallas_call(
        functools.partial(kernel, counts),
        out_shape=(shape, shape),
        in_specs=[any_spec, any_spec, any_spec, vmem, any_spec],
        out_specs=(vmem, vmem),
        scratch_shapes=[
            pltpu.VMEM((FIELDS + 1, wide, tall, long), f32),
            pltpu.VMEM((ITERS + 1, wide, tall, long), f32),
            pltpu.VMEM((2, wide, tall, long), f32),
            pltpu.VMEM((wide, tall, long), f32),
            pltpu.VMEM((SUB, LANES), f32),
            pltpu.VMEM((2, nx, ny, nz), jnp.int32),
            pltpu.VMEM((nx, ny, nz), f32),
            pltpu.VMEM((2, nx, ny, nz), f32),
            pltpu.VMEM((1, LANES), f32),
            pltpu.VMEM((devices, 1, LANES), f32),
            pltpu.VMEM((1, LANES), f32),
            pltpu.VMEM((devices, 1, LANES), f32),
            pltpu.SemaphoreType.DMA((4,)),
            pltpu.SemaphoreType.DMA((8,)),
            pltpu.SemaphoreType.DMA((8,)),
            pltpu.SemaphoreType.DMA((8,)),
            pltpu.SemaphoreType.DMA((8,)),
            pltpu.SemaphoreType.DMA((2,)),
            pltpu.SemaphoreType.DMA((2,)),
            pltpu.SemaphoreType.DMA((2,)),
            pltpu.SemaphoreType.DMA((2,)),
        ],
        compiler_params=pltpu.CompilerParams(collective_id=0, has_side_effects=True),
    )(warm, source, category, table, flags)


def solution(mesh):
    counts = tuple(mesh.shape[a] for a in AXES)
    spec = P("gx", "gy", "gz")
    return jax.shard_map(
        functools.partial(body, counts),
        mesh=mesh,
        in_specs=(spec, spec, spec, P(), spec),
        out_specs=(spec, spec),
        check_vma=False,
    )
```

time: 343 us -> 37.1 us (0.11)
  blocking collectives: 156 us -> 0 us
  waiting for transfers between devices: 92.3 us -> 0 us
  starting transfers between devices: 67.6 us -> 0 us
  Pallas kernels: 0 us -> 33 us
  between operations: 15.1 us -> 0.65 us
  other arithmetic: 8.92 us -> 0 us
    psum x4 -> x0, blocking collectives: 156 us -> none  [two_products(): lax.psum((jnp.sum(remaining_mismatch * remaining_mismatch), jnp.sum(remai...]
    ppermute x36 -> x0, waiting for transfers between devices: 92.3 us -> none  [the longest x18 67.7 us: padded_2(): lax.ppermute(head, axis, [((i + 1) % count, i) for i in range(ends)])]
    ppermute x36 -> x0, starting transfers between devices: 67.6 us -> none  [the longest x18 44.3 us: padded_2(): lax.ppermute(tail, axis, [(i, (i + 1) % count) for i in range(ends)])]
    pallas_call x0 -> x1, Pallas kernels: none -> 33 us  [body(): pl.pallas_call(functools.partial(kernel, counts), out_shape=(shape, shape...]
    reduce_sum x5 -> x0, other arithmetic: 4.7 us -> none  [the longest x4 3.68 us: two_products(): jnp.sum(remaining_mismatch * image)]
  transfers between devices with their start and end apart: 36 -> 0, of which waited for: 27 -> 0; matrix products, arithmetic and copies ran while one was open for 0% -> 0% of each run, Pallas kernels for 0% -> 0%
where the time goes in v1:
time: 37.1 us; the launch traced here: 37 us
  Pallas kernels  33 us (89%)
  local copies, waits for them, and re-layouts  3.31 us (9%)
  between operations  0.65 us (2%)
    pallas_call x1, Pallas kernels, body(): pl.pallas_call(functools.partial(kernel, counts), out_shape=(shape, shape...  33 us
    unnamed x4, local copies, waits for them, and re-layouts  2.14 us
    broadcast_in_dim x1, local copies, waits for them, and re-layouts, body(): table = jnp.pad(table, (0, LANES - table.shape[0]))[None]  1.17 us

profile of v1, /device:TPU:0, one launch (start us, length us, event | category | flops | bytes accessed | tf_op | source)
XLA Modules:
  0.0 37.0 jit_solution(8604210335165052704)
XLA Ops:
  0.6 1.2 %pad_bitcast_fusion.table_in = f32[1,128]{1,0:T(1,128)} fusion(f32[16]{0:T(128)} %param.8), kind=kLoop, calls=%fused_computation | loop fusion | bytes 576 | tf_op jit(solution)/shard_map/broadcast_in_dim | solution.py:416
  1.8 33.0 %shard_map.68 = (f32[8,16,128]{2,1,0:T(8,128)}, f32[8,16,128]{2,1,0:T(8,128)}) custom-call(f32[8,16,128]{2,1,0:T(8,128)} %warm_in.1, f32[8,16,128]{2,1,0:T(8,128)} %source_in.1, s32[8,16,128]{2,1,0:T(8,128)} %category_in.1, f32[1,128]{1,0:T(1,128)} %pad_bitcast_fusion.table_in, s32[8,16,128]{2,1,0:T(8,128)} %flags_in.1), custom_call_target="tpu_custom_call" | custom-call | tf_op jit(solution)/shard_map/pallas_call | solution.py:421
  34.8 0.0 copy-start
  34.8 1.5 %copy.9 = f32[8,16,128]{2,1,0:T(8,128)} copy(f32[8,16,128]{2,1,0:T(8,128)} %get-tuple-element.4) | data formatting | bytes 131072
  36.3 0.0 copy-done
  36.3 0.6 %copy.10 = f32[8,16,128]{2,1,0:T(8,128)} copy(f32[8,16,128]{2,1,0:T(8,128)S(1)} %copy-done) | data formatting | bytes 131072
Async XLA Ops:
  34.8 1.5 %copy-start = (f32[8,16,128]{2,1,0:T(8,128)S(1)}, f32[8,16,128]{2,1,0:T(8,128)}, u32[]{:S(2)}) copy-start(f32[8,16,128]{2,1,0:T(8,128)} %get-tuple-element.5) | copy-start | bytes 196612

commit v2 on v1

--- a/solution.py
+++ b/solution.py
@@ -23,8 +23,7 @@
 
 def smooth(values, axis):
     size = values.shape[axis]
-    once = values + pltpu.roll(values, 1, axis)
-    return once + pltpu.roll(once, size - 1, axis)
+    return (values + values) + (pltpu.roll(values, 1, axis) + pltpu.roll(values, size - 1, axis))
 
 
 def smooth_all(before, center, after):
@@ -43,15 +42,17 @@
     grid,
     basis,
     flux,
+    warm_flux,
     diag,
+    couple,
     table,
+    table_row,
     ints,
     edges,
     beside,
-    bound_row,
-    bound_rows,
-    gram_row,
-    gram_rows,
+    row_out,
+    plane_rows,
+    line_rows,
     load_sems,
     raw_send,
     raw_recv,
@@ -62,21 +63,21 @@
     row_send,
     row_recv,
 ):
-    devices = counts[0] * counts[1] * counts[2]
+    plane, line = counts[0] * counts[1], counts[2]
     nx, ny, nz = warm_out.shape
     depth = ITERS + 1
     wide, tall, long = grid.shape[1:]
+    short = ny + SUB
     here = [lax.axis_index(a) for a in AXES]
-    me = (here[0] * counts[1] + here[1]) * counts[2] + here[2]
-
-    def at(linear):
-        return {
-            "gx": linear // (counts[1] * counts[2]),
-            "gy": (linear // counts[2]) % counts[1],
-            "gz": linear % counts[2],
-        }
-
-    main = (slice(depth, depth + nx), slice(0, ny), slice(0, nz))
+    in_plane = here[0] * counts[1] + here[1]
+    plane_targets = [
+        {"gx": other // counts[1], "gy": other % counts[1], "gz": here[2]}
+        for other in [(in_plane + step) % plane for step in range(1, plane)]
+    ]
+    line_targets = [
+        {"gx": here[0], "gy": here[1], "gz": (here[2] + step) % line} for step in range(1, line)
+    ]
+
     loads = [
         pltpu.make_async_copy(category_in, ints.at[0], load_sems.at[0]),
         pltpu.make_async_copy(flags_in, ints.at[1], load_sems.at[1]),
@@ -86,8 +87,9 @@
         pltpu.make_async_copy(
             source_in, grid.at[SOURCE, pl.ds(depth, nx), pl.ds(0, ny), pl.ds(0, nz)], load_sems.at[3]
         ),
+        pltpu.make_async_copy(table_in, table_row, load_sems.at[4]),
     ]
-    for load in loads[:2]:
+    for load in loads:
         load.start()
 
     for f in range(FIELDS + 1):
@@ -95,21 +97,17 @@
         grid[f, depth + nx :, :, 0:nz] = jnp.zeros((depth, tall, nz), jnp.float32)
         grid[f, depth : depth + nx, ny:, 0:nz] = jnp.zeros((nx, tall - ny, nz), jnp.float32)
     beside[...] = jnp.zeros(beside.shape, jnp.float32)
-    for load in loads[2:]:
-        load.start()
-
+    table[...] = jnp.zeros(table.shape, jnp.float32)
     barrier = pltpu.get_barrier_semaphore()
 
-    @pl.loop(1, devices)
-    def _(step):
-        pl.semaphore_signal(
-            barrier, inc=1, device_id=at((me + step) % devices), device_id_type=MESH
-        )
+    for target in plane_targets + line_targets:
+        pl.semaphore_signal(barrier, inc=1, device_id=target, device_id_type=MESH)
 
     for load in loads:
         load.wait()
 
-    lookup = jnp.broadcast_to(table_in[...], (ny, LANES))
+    table[0:1, 0 : table_in.shape[1]] = table_row[...]
+    lookup = jnp.broadcast_to(table[0:1, :], (ny, LANES))
     lane = lax.broadcasted_iota(jnp.int32, (ny, LANES), 1)
     top = jnp.zeros((ny, LANES), jnp.float32)
     total = jnp.zeros((ny, LANES), jnp.float32)
@@ -142,10 +140,10 @@
     low = 1.0 + interval_delta * cooling * shrink(jnp.min, least)
     row_lane = lax.broadcasted_iota(jnp.int32, (1, LANES), 1)
     row = jnp.where(row_lane == 0, high, -low)
-    bound_row[...] = row
-    bound_rows[me] = row
-
-    pl.semaphore_wait(barrier, devices - 1)
+    row_out[0] = row
+    plane_rows[0, in_plane] = row
+
+    pl.semaphore_wait(barrier, plane + line - 2)
 
     def remote(src, dst, send, recv, offset):
         return pltpu.make_async_remote_copy(
@@ -175,32 +173,29 @@
         z_copies.append((copy, dz))
         pl.when(exists((0, 0, dz)))(copy.start)
 
-    def spread(row_ref, rows_ref, k):
-        @pl.loop(1, devices)
-        def _(step):
+    def share(stage, rows_ref, slot, targets):
+        for target in targets:
             pltpu.make_async_remote_copy(
-                src_ref=row_ref,
-                dst_ref=rows_ref.at[me],
-                send_sem=row_send.at[k],
-                recv_sem=row_recv.at[k],
-                device_id=at((me + step) % devices),
+                src_ref=row_out.at[stage],
+                dst_ref=rows_ref.at[slot],
+                send_sem=row_send.at[stage],
+                recv_sem=row_recv.at[stage],
+                device_id=target,
                 device_id_type=MESH,
             ).start()
 
-    def spread_wait(rows_ref, k):
-        whole = pltpu.make_async_remote_copy(
-            src_ref=rows_ref.at[pl.ds(0, devices - 1)],
-            dst_ref=rows_ref.at[pl.ds(0, devices - 1)],
-            send_sem=row_send.at[k],
-            recv_sem=row_recv.at[k],
-            device_id=at((me + 1) % devices),
-            device_id_type=MESH,
-        )
-        whole.wait_send()
-        whole.wait_recv()
-
-    if devices > 1:
-        spread(bound_row, bound_rows, 0)
+    def share_wait(stage, rows_ref, targets):
+        if targets:
+            whole = pltpu.make_async_remote_copy(
+                src_ref=rows_ref.at[pl.ds(0, len(targets))],
+                dst_ref=rows_ref.at[pl.ds(0, len(targets))],
+                send_sem=row_send.at[stage],
+                recv_sem=row_recv.at[stage],
+                device_id=targets[0],
+                device_id_type=MESH,
+            )
+            whole.wait_send()
+            whole.wait_recv()
 
     def ranges(offset):
         dx, dy = offset
@@ -244,6 +239,8 @@
     for copy, (dx, dy) in raw:
         pl.when(exists((dx, dy, 0)))(copy.start)
 
+    share(0, plane_rows.at[0], in_plane, plane_targets)
+
     for copy, dz in z_copies:
         pl.when(exists((0, 0, -dz)))(copy.wait_recv)
     low_half = lane % SLOT < SLOT // 2
@@ -252,77 +249,96 @@
     for copy, (dx, dy) in fwd:
         pl.when(exists((dx, dy, 0)))(copy.start)
 
+    share_wait(0, plane_rows.at[0], plane_targets)
+    row = jnp.max(plane_rows[0], axis=0)
+    row_out[1] = row
+    line_rows[0, here[2]] = row
+    share(1, line_rows.at[0], here[2], line_targets)
+
     for copy, (dx, dy) in raw:
         pl.when(exists((-dx, -dy, 0)))(copy.wait_recv)
     for copy, (dx, dy) in fwd:
         pl.when(exists((-dx, -dy, 0)))(copy.wait_recv)
 
-    for i in range(wide):
-        packed = grid[EDGES, i, :, 0:nz]
-        for f in range(FIELDS):
-            grid[f, i, :, nz:] = pltpu.roll(packed, (-f * SLOT - SLOT // 2) % LANES, 1)
-        flux[0, i] = grid[COND, i] * grid[WARM, i]
-
-    if devices > 1:
-        spread_wait(bound_rows, 0)
-    bounds = jnp.max(bound_rows[...], axis=0)
+    @pl.loop(0, wide // 2)
+    def _(pair):
+        for u in range(2):
+            i = 2 * pair + u
+            packed = grid[EDGES, i, :, 0:nz]
+            for f in range(FIELDS):
+                grid[f, i, :, nz:] = pltpu.roll(packed, (-f * SLOT - SLOT // 2) % LANES, 1)
+            warm_flux[i] = grid[COND, i] * grid[WARM, i]
+
+    share_wait(1, line_rows.at[0], line_targets)
+    bounds = jnp.max(line_rows[0], axis=0)
     pick = lambda v, i: jnp.sum(jnp.where(row_lane == i, v, 0.0), axis=1, keepdims=True)
     high, low = pick(bounds, 0), -pick(bounds, 1)
     middle = 0.5 * (high + low)
     half = 0.5 * (high - low)
-    scale = 1.0 / half
-
-    def valid(index, size, k):
+    twice = 2.0 / half
+
+    def valid(index, size, cut, k):
         inner = index < size
-        right = jnp.logical_and(index < size + (SUB if k == 1 else LANES // 2), here[k] < counts[k] - 1)
-        left = jnp.logical_and(index >= size + (SUB if k == 1 else LANES // 2), here[k] > 0)
+        right = jnp.logical_and(index < size + cut, here[k] < counts[k] - 1)
+        left = jnp.logical_and(index >= size + cut, here[k] > 0)
         return jnp.logical_or(inner, jnp.logical_or(right, left))
 
-    y_index = lax.broadcasted_iota(jnp.int32, (tall, long), 0)
-    z_index = lax.broadcasted_iota(jnp.int32, (tall, long), 1)
-    inside = jnp.where(
-        jnp.logical_and(valid(y_index, ny, 1), valid(z_index, nz, 2)), 0.125 * interval_delta, 0.0
-    )
+    def inside_of(rows, cut):
+        y_index = lax.broadcasted_iota(jnp.int32, (rows, long), 0)
+        z_index = lax.broadcasted_iota(jnp.int32, (rows, long), 1)
+        both = jnp.logical_and(valid(y_index, ny, cut, 1), valid(z_index, nz, LANES // 2, 2))
+        return jnp.where(both, 1.0, 0.0)
+
     x_left = jnp.where(here[0] > 0, 1.0, 0.0)
     x_right = jnp.where(here[0] < counts[0] - 1, 1.0, 0.0)
 
-    def mask(i):
-        if i < depth:
-            return inside * x_left
-        if i >= depth + nx:
-            return inside * x_right
-        return inside
+    def x_inside(i):
+        return jnp.where(i < depth, x_left, jnp.where(i >= depth + nx, x_right, 1.0))
 
     quarter = 0.125 * interval_delta
-
-    for i in range(1, wide - 1):
-        cond = grid[COND, i]
-        ring = smooth_all(grid[COND, i - 1], cond, grid[COND, i + 1])
-        d = 1.0 + interval_delta * cooling * grid[FLAGS, i] + 8.0 * interval_delta * cond + quarter * ring
-        diag[i] = d
-        warm = grid[WARM, i]
-        own = smooth_all(grid[WARM, i - 1], warm, grid[WARM, i + 1])
-        push = smooth_all(flux[0, i - 1], flux[0, i], flux[0, i + 1])
-        image = d * warm - (quarter * cond * own + mask(i) * push)
-        left = warm + interval_delta * grid[SOURCE, i] - image
-        basis[0, i] = left
-        flux[1, i] = cond * left
-
+    inside = quarter * inside_of(tall, SUB)
+    first_half = lax.broadcasted_iota(jnp.int32, (SUB, long), 0) < SUB // 2
+
+    def narrow(v):
+        ends = jnp.where(first_half, v[ny : ny + SUB], v[ny + SUB :])
+        return jnp.concatenate([v[:ny], ends], axis=0)
+
+    @pl.loop(0, (wide - 2) // 2)
+    def _(pair):
+        for u in range(2):
+            i = 1 + 2 * pair + u
+            cond = grid[COND, i]
+            ring = smooth_all(grid[COND, i - 1], cond, grid[COND, i + 1])
+            d = 1.0 + interval_delta * cooling * grid[FLAGS, i]
+            d = d + 8.0 * interval_delta * cond + quarter * ring
+            warm = grid[WARM, i]
+            own = smooth_all(grid[WARM, i - 1], warm, grid[WARM, i + 1])
+            push = smooth_all(warm_flux[i - 1], warm_flux[i], warm_flux[i + 1])
+            image = d * warm - (quarter * cond * own + x_inside(i) * inside * push)
+            left = narrow(warm + interval_delta * grid[SOURCE, i] - image)
+            edge = (quarter * twice) * narrow(cond)
+            basis[0, i] = left
+            diag[i] = twice * (narrow(d) - middle)
+            couple[i] = edge
+            flux[0, i] = edge * left
+
+    within = inside_of(short, SUB // 2)
     for k in range(ITERS):
-        now, later = (k + 1) % 2, k % 2
-        for i in range(2 + k, wide - 2 - k):
-            cond = grid[COND, i]
-            mid = basis[k, i]
-            own = smooth_all(basis[k, i - 1], mid, basis[k, i + 1])
-            push = smooth_all(flux[now, i - 1], flux[now, i], flux[now, i + 1])
-            image = (diag[i] - middle) * mid - (quarter * cond * own + mask(i) * push)
-            if k == 0:
-                fresh = scale * image
-            else:
-                fresh = (2.0 * scale) * image - basis[k - 1, i]
-            basis[k + 1, i] = fresh
-            if k + 1 < ITERS:
-                flux[later, i] = cond * fresh
+
+        @pl.loop(0, (wide - 4 - 2 * k) // 2)
+        def _(pair):
+            for u in range(2):
+                i = 2 + k + 2 * pair + u
+                edge = couple[i]
+                mid = basis[k, i]
+                own = smooth_all(basis[k, i - 1], mid, basis[k, i + 1])
+                push = smooth_all(flux[k % 2, i - 1], flux[k % 2, i], flux[k % 2, i + 1])
+                fresh = diag[i] * mid - (edge * own + x_inside(i) * within * push)
+                if k > 0:
+                    fresh = fresh - basis[k - 1, i]
+                basis[k + 1, i] = fresh
+                if k + 1 < ITERS:
+                    flux[(k + 1) % 2, i] = edge * fresh
 
     sums = [None] * len(PAIRS)
     for i in range(depth, depth + nx):
@@ -340,24 +356,25 @@
         column = jnp.sum(tile, axis=1, keepdims=True)
         row = row + jnp.where(across == diagonal + start, column, 0.0)
     row = jnp.sum(row, axis=0, keepdims=True)
-    gram_row[...] = row
-    gram_rows[me] = row
-    if devices > 1:
-        spread(gram_row, gram_rows, 1)
-        spread_wait(gram_rows, 1)
-    row = jnp.sum(gram_rows[...], axis=0)
+    row_out[2] = row
+    plane_rows[1, in_plane] = row
+    share(2, plane_rows.at[1], in_plane, plane_targets)
+    share_wait(2, plane_rows.at[1], plane_targets)
+    row = jnp.sum(plane_rows[1], axis=0)
+    row_out[3] = row
+    line_rows[1, here[2]] = row
+    share(3, line_rows.at[1], here[2], line_targets)
+    share_wait(3, line_rows.at[1], line_targets)
+    row = jnp.sum(line_rows[1], axis=0)
     gram = {}
     for n, (a, b) in enumerate(PAIRS):
         gram[a, b] = gram[b, a] = pick(row, n)
 
     def apply(p):
-        q = [middle * a for a in p] + [None]
-        q[len(p)] = jnp.zeros_like(half)
+        q = [middle * a for a in p] + [jnp.zeros_like(half)]
         for i, a in enumerate(p):
-            if i == 0:
-                q[1] = q[1] + half * a
-            else:
-                q[i + 1] = q[i + 1] + (0.5 * half) * a
+            q[i + 1] = q[i + 1] + (0.5 * half) * a
+            if i > 0:
                 q[i - 1] = q[i - 1] + (0.5 * half) * a
         return q
 
@@ -411,9 +428,11 @@
 def body(counts, warm, source, category, table, flags):
     nx, ny, nz = warm.shape
     depth = ITERS + 1
-    devices = counts[0] * counts[1] * counts[2]
-    wide, tall, long = nx + 2 * depth, ny + 2 * SUB, nz + LANES
-    table = jnp.pad(table, (0, LANES - table.shape[0]))[None]
+    plane, line = counts[0] * counts[1], counts[2]
+    if nx < depth or nx % 2 or ny % SUB or nz != LANES or table.shape[0] > LANES:
+        raise ValueError("block shape")
+    wide, tall, short, long = nx + 2 * depth, ny + 2 * SUB, ny + SUB, nz + LANES
+    table = table[None]
     any_spec = pl.BlockSpec(memory_space=pl.ANY)
     vmem = pl.BlockSpec(memory_space=pltpu.VMEM)
     shape = jax.ShapeDtypeStruct(warm.shape, jnp.float32)
@@ -421,30 +440,32 @@
     return pl.pallas_call(
         functools.partial(kernel, counts),
         out_shape=(shape, shape),
-        in_specs=[any_spec, any_spec, any_spec, vmem, any_spec],
+        in_specs=[any_spec] * 5,
         out_specs=(vmem, vmem),
         scratch_shapes=[
             pltpu.VMEM((FIELDS + 1, wide, tall, long), f32),
-            pltpu.VMEM((ITERS + 1, wide, tall, long), f32),
-            pltpu.VMEM((2, wide, tall, long), f32),
+            pltpu.VMEM((ITERS + 1, wide, short, long), f32),
+            pltpu.VMEM((2, wide, short, long), f32),
             pltpu.VMEM((wide, tall, long), f32),
+            pltpu.VMEM((wide, short, long), f32),
+            pltpu.VMEM((wide, short, long), f32),
             pltpu.VMEM((SUB, LANES), f32),
+            pltpu.VMEM(table.shape, f32),
             pltpu.VMEM((2, nx, ny, nz), jnp.int32),
             pltpu.VMEM((nx, ny, nz), f32),
             pltpu.VMEM((2, nx, ny, nz), f32),
-            pltpu.VMEM((1, LANES), f32),
-            pltpu.VMEM((devices, 1, LANES), f32),
-            pltpu.VMEM((1, LANES), f32),
-            pltpu.VMEM((devices, 1, LANES), f32),
-            pltpu.SemaphoreType.DMA((4,)),
+            pltpu.VMEM((4, 1, LANES), f32),
+            pltpu.VMEM((2, plane, 1, LANES), f32),
+            pltpu.VMEM((2, line, 1, LANES), f32),
+            pltpu.SemaphoreType.DMA((5,)),
             pltpu.SemaphoreType.DMA((8,)),
             pltpu.SemaphoreType.DMA((8,)),
             pltpu.SemaphoreType.DMA((8,)),
             pltpu.SemaphoreType.DMA((8,)),
             pltpu.SemaphoreType.DMA((2,)),
             pltpu.SemaphoreType.DMA((2,)),
-            pltpu.SemaphoreType.DMA((2,)),
-            pltpu.SemaphoreType.DMA((2,)),
+            pltpu.SemaphoreType.DMA((4,)),
+            pltpu.SemaphoreType.DMA((4,)),
         ],
         compiler_params=pltpu.CompilerParams(collective_id=0, has_side_effects=True),
     )(warm, source, category, table, flags)

time: 37.1 us -> 32.1 us (0.87)
  Pallas kernels: 33 us -> 29.1 us
  local copies, waits for them, and re-layouts: 3.31 us -> 2.14 us
    pallas_call x1, Pallas kernels: 33 us -> 29.1 us  [body(): pl.pallas_call(functools.partial(kernel, counts), out_shape=(shape, shape...]
    broadcast_in_dim x1 -> x0, local copies, waits for them, and re-layouts: 1.17 us -> none  [body(): table = jnp.pad(table, (0, LANES - table.shape[0]))[None]]
where the time goes in v2:
time: 32.1 us; the launch traced here: 31.9 us
  Pallas kernels  29.1 us (91%)
  local copies, waits for them, and re-layouts  2.14 us (7%)
  between operations  0.65 us (2%)
    pallas_call x1, Pallas kernels, body(): pl.pallas_call(functools.partial(kernel, counts), out_shape=(shape, shape...  29.1 us
    unnamed x4, local copies, waits for them, and re-layouts  2.14 us

profile of v2, /device:TPU:0, one launch (start us, length us, event | category | flops | bytes accessed | tf_op | source)
XLA Modules:
  0.0 31.9 jit_solution(17418955789098662179)
XLA Ops:
  0.6 29.1 %shard_map.68 = (f32[8,16,128]{2,1,0:T(8,128)}, f32[8,16,128]{2,1,0:T(8,128)}) custom-call(f32[8,16,128]{2,1,0:T(8,128)} %warm_in.1, f32[8,16,128]{2,1,0:T(8,128)} %source_in.1, s32[8,16,128]{2,1,0:T(8,128)} %category_in.1, f32[1,16]{1,0:T(1,128)} %bitcast.1, s32[8,16,128]{2,1,0:T(8,128)} %flags_in.1), custom_call_target="tpu_custom_call" | custom-call | tf_op jit(solution)/shard_map/pallas_call | solution.py:440
  29.8 0.0 copy-start
  29.8 1.5 %copy.9 = f32[8,16,128]{2,1,0:T(8,128)} copy(f32[8,16,128]{2,1,0:T(8,128)} %get-tuple-element.4) | data formatting | bytes 131072
  31.3 0.0 copy-done
  31.3 0.6 %copy.10 = f32[8,16,128]{2,1,0:T(8,128)} copy(f32[8,16,128]{2,1,0:T(8,128)S(1)} %copy-done) | data formatting | bytes 131072
Async XLA Ops:
  29.8 1.5 %copy-start = (f32[8,16,128]{2,1,0:T(8,128)S(1)}, f32[8,16,128]{2,1,0:T(8,128)}, u32[]{:S(2)}) copy-start(f32[8,16,128]{2,1,0:T(8,128)} %get-tuple-element.5) | copy-start | bytes 196612

commit v3 on v2

--- a/solution.py
+++ b/solution.py
@@ -14,9 +14,10 @@
 MESH = pl.DeviceIdType.MESH
 AXES = ("gx", "gy", "gz")
 SUB = 8
+DIRECT = 64
 LANES = 128
 FIELDS = 4
-WARM, SOURCE, COND, FLAGS, EDGES = range(5)
+WARM, COND, SOURCE, FLAGS, EDGES = range(5)
 SLOT = LANES // FIELDS
 PAIRS = [(i, j) for i in range(ITERS + 1) for j in range(i, ITERS + 1) if i < ITERS]
 
@@ -49,13 +50,17 @@
     table_row,
     ints,
     edges,
+    mixed,
     beside,
     row_out,
     plane_rows,
     line_rows,
+    all_rows,
     load_sems,
     raw_send,
     raw_recv,
+    mix_send,
+    mix_recv,
     fwd_send,
     fwd_recv,
     z_send,
@@ -98,6 +103,15 @@
         grid[f, depth : depth + nx, ny:, 0:nz] = jnp.zeros((nx, tall - ny, nz), jnp.float32)
     beside[...] = jnp.zeros(beside.shape, jnp.float32)
     table[...] = jnp.zeros(table.shape, jnp.float32)
+    moved_by = [[(here[k] + step) % counts[k] for step in range(counts[k])] for k in range(3)]
+    all_targets = [
+        {"gx": moved_by[0][a], "gy": moved_by[1][b], "gz": moved_by[2][c]}
+        for c in reversed(range(counts[2]))
+        for b in reversed(range(counts[1]))
+        for a in reversed(range(counts[0]))
+        if a or b or c
+    ]
+
     barrier = pltpu.get_barrier_semaphore()
 
     for target in plane_targets + line_targets:
@@ -120,8 +134,8 @@
         grid[FLAGS, depth + i, 0:ny, 0:nz] = flag
         pieces = [
             grid[WARM, depth + i, 0:ny, 0:nz],
+            cond,
             grid[SOURCE, depth + i, 0:ny, 0:nz],
-            cond,
             flag,
         ]
         packed = None
@@ -129,6 +143,14 @@
             turned = pltpu.roll(piece, (f * SLOT + SLOT // 2) % LANES, 1)
             packed = turned if packed is None else jnp.where(lane // SLOT == f, turned, packed)
         edges[i] = packed
+        upper = lax.broadcasted_iota(jnp.int32, (SUB, nz), 0) < SUB // 2
+        last, first = slice(ny - SUB, ny), slice(0, SUB)
+        mixed[0, i] = jnp.where(
+            upper, pltpu.roll(flag[last], SUB // 2, 0), grid[SOURCE, depth + i, last, 0:nz]
+        )
+        mixed[1, i] = jnp.where(
+            upper, grid[SOURCE, depth + i, first, 0:nz], pltpu.roll(flag[first], SUB // 2, 0)
+        )
         top = jnp.maximum(top, cond)
         total = total + cond
         most = jnp.maximum(most, flag)
@@ -216,26 +238,42 @@
 
     offsets = [(0, 1), (0, -1), (1, 1), (-1, -1), (1, -1), (-1, 1), (1, 0), (-1, 0)]
 
-    def around(fields, sends, recvs):
-        copies = []
-        for k, offset in enumerate(offsets):
-            src, dst = ranges(offset)
-            copies.append(
+    raw, fwd = [], []
+    for k, offset in enumerate(offsets):
+        src, dst = ranges(offset)
+        full = offset + (0,)
+        count = FIELDS if offset[1] == 0 else SOURCE
+        fields = (pl.ds(0, count),)
+        raw.append(
+            (
+                remote(
+                    grid.at[fields + src], grid.at[fields + dst], raw_send.at[k], raw_recv.at[k], full
+                ),
+                offset,
+            )
+        )
+        if offset[1] != 0:
+            xs = pl.ds(src[0].start - depth, src[0].size)
+            raw.append(
                 (
                     remote(
-                        grid.at[(fields,) + src],
-                        grid.at[(fields,) + dst],
-                        sends.at[k],
-                        recvs.at[k],
-                        offset + (0,),
+                        mixed.at[0 if offset[1] > 0 else 1, xs],
+                        grid.at[(SOURCE,) + dst],
+                        mix_send.at[k],
+                        mix_recv.at[k],
+                        full,
                     ),
                     offset,
                 )
             )
-        return copies
-
-    raw = around(pl.ds(0, FIELDS), raw_send, raw_recv)
-    fwd = around(pl.ds(EDGES, 1), fwd_send, fwd_recv)
+        fwd.append(
+            (
+                remote(
+                    grid.at[(EDGES,) + src], grid.at[(EDGES,) + dst], fwd_send.at[k], fwd_recv.at[k], full
+                ),
+                offset,
+            )
+        )
     for copy, (dx, dy) in raw:
         pl.when(exists((dx, dy, 0)))(copy.start)
 
@@ -260,11 +298,20 @@
     for copy, (dx, dy) in fwd:
         pl.when(exists((-dx, -dy, 0)))(copy.wait_recv)
 
-    @pl.loop(0, wide // 2)
-    def _(pair):
-        for u in range(2):
-            i = 2 * pair + u
+    batch = next(u for u in (6, 4, 2) if wide % u == 0)
+
+    @pl.loop(0, wide // batch)
+    def _(group):
+        for u in range(batch):
+            i = batch * group + u
             packed = grid[EDGES, i, :, 0:nz]
+            grid[FLAGS, i, ny:, 0:nz] = jnp.concatenate(
+                [
+                    pltpu.roll(grid[SOURCE, i, ny : ny + SUB, 0:nz], SUB // 2, 0),
+                    pltpu.roll(grid[SOURCE, i, ny + SUB :, 0:nz], SUB // 2, 0),
+                ],
+                axis=0,
+            )
             for f in range(FIELDS):
                 grid[f, i, :, nz:] = pltpu.roll(packed, (-f * SLOT - SLOT // 2) % LANES, 1)
             warm_flux[i] = grid[COND, i] * grid[WARM, i]
@@ -303,10 +350,12 @@
         ends = jnp.where(first_half, v[ny : ny + SUB], v[ny + SUB :])
         return jnp.concatenate([v[:ny], ends], axis=0)
 
-    @pl.loop(0, (wide - 2) // 2)
-    def _(pair):
-        for u in range(2):
-            i = 1 + 2 * pair + u
+    several = next(u for u in (4, 2) if (wide - 2) % u == 0)
+
+    @pl.loop(0, (wide - 2) // several)
+    def _(group):
+        for u in range(several):
+            i = 1 + several * group + u
             cond = grid[COND, i]
             ring = smooth_all(grid[COND, i - 1], cond, grid[COND, i + 1])
             d = 1.0 + interval_delta * cooling * grid[FLAGS, i]
@@ -325,10 +374,12 @@
     within = inside_of(short, SUB // 2)
     for k in range(ITERS):
 
-        @pl.loop(0, (wide - 4 - 2 * k) // 2)
-        def _(pair):
-            for u in range(2):
-                i = 2 + k + 2 * pair + u
+        half_planes = wide // 2 - 2 - k
+
+        @pl.loop(0, 2)
+        def _(group):
+            for u in range(half_planes):
+                i = 2 + k + half_planes * group + u
                 edge = couple[i]
                 mid = basis[k, i]
                 own = smooth_all(basis[k, i - 1], mid, basis[k, i + 1])
@@ -357,15 +408,22 @@
         row = row + jnp.where(across == diagonal + start, column, 0.0)
     row = jnp.sum(row, axis=0, keepdims=True)
     row_out[2] = row
-    plane_rows[1, in_plane] = row
-    share(2, plane_rows.at[1], in_plane, plane_targets)
-    share_wait(2, plane_rows.at[1], plane_targets)
-    row = jnp.sum(plane_rows[1], axis=0)
-    row_out[3] = row
-    line_rows[1, here[2]] = row
-    share(3, line_rows.at[1], here[2], line_targets)
-    share_wait(3, line_rows.at[1], line_targets)
-    row = jnp.sum(line_rows[1], axis=0)
+    if plane * line <= DIRECT:
+        mine = in_plane * line + here[2]
+        all_rows[mine] = row
+        share(2, all_rows, mine, all_targets)
+        share_wait(2, all_rows, all_targets)
+        row = jnp.sum(all_rows[...], axis=0)
+    else:
+        plane_rows[1, in_plane] = row
+        share(2, plane_rows.at[1], in_plane, plane_targets)
+        share_wait(2, plane_rows.at[1], plane_targets)
+        row = jnp.sum(plane_rows[1], axis=0)
+        row_out[3] = row
+        line_rows[1, here[2]] = row
+        share(3, line_rows.at[1], here[2], line_targets)
+        share_wait(3, line_rows.at[1], line_targets)
+        row = jnp.sum(line_rows[1], axis=0)
     gram = {}
     for n, (a, b) in enumerate(PAIRS):
         gram[a, b] = gram[b, a] = pick(row, n)
@@ -453,11 +511,15 @@
             pltpu.VMEM(table.shape, f32),
             pltpu.VMEM((2, nx, ny, nz), jnp.int32),
             pltpu.VMEM((nx, ny, nz), f32),
+            pltpu.VMEM((2, nx, SUB, nz), f32),
             pltpu.VMEM((2, nx, ny, nz), f32),
             pltpu.VMEM((4, 1, LANES), f32),
             pltpu.VMEM((2, plane, 1, LANES), f32),
             pltpu.VMEM((2, line, 1, LANES), f32),
+            pltpu.VMEM((plane * line, 1, LANES), f32),
             pltpu.SemaphoreType.DMA((5,)),
+            pltpu.SemaphoreType.DMA((8,)),
+            pltpu.SemaphoreType.DMA((8,)),
             pltpu.SemaphoreType.DMA((8,)),
             pltpu.SemaphoreType.DMA((8,)),
             pltpu.SemaphoreType.DMA((8,)),

time: 32.1 us -> 27.9 us (0.87)
  Pallas kernels: 29.1 us -> 24.9 us
    pallas_call x1, Pallas kernels: 29.1 us -> 24.9 us  [body(): pl.pallas_call(functools.partial(kernel, counts), out_shape=(shape, shape...]
where the time goes in v3:
time: 27.9 us; the launch traced here: 27.7 us
  Pallas kernels  24.9 us (89%)
  local copies, waits for them, and re-layouts  2.14 us (8%)
  between operations  0.65 us (2%)
    pallas_call x1, Pallas kernels, body(): pl.pallas_call(functools.partial(kernel, counts), out_shape=(shape, shape...  24.9 us
    unnamed x4, local copies, waits for them, and re-layouts  2.14 us

profile of v3, /device:TPU:0, one launch (start us, length us, event | category | flops | bytes accessed | tf_op | source)
XLA Modules:
  0.0 27.7 jit_solution(13462485786859112586)
XLA Ops:
  0.6 24.9 %shard_map.68 = (f32[8,16,128]{2,1,0:T(8,128)}, f32[8,16,128]{2,1,0:T(8,128)}) custom-call(f32[8,16,128]{2,1,0:T(8,128)} %warm_in.1, f32[8,16,128]{2,1,0:T(8,128)} %source_in.1, s32[8,16,128]{2,1,0:T(8,128)} %category_in.1, f32[1,16]{1,0:T(1,128)} %bitcast.1, s32[8,16,128]{2,1,0:T(8,128)} %flags_in.1), custom_call_target="tpu_custom_call" | custom-call | tf_op jit(solution)/shard_map/pallas_call | solution.py:498
  25.5 0.0 copy-start
  25.5 1.5 %copy.9 = f32[8,16,128]{2,1,0:T(8,128)} copy(f32[8,16,128]{2,1,0:T(8,128)} %get-tuple-element.4) | data formatting | bytes 131072
  27.0 0.0 copy-done
  27.0 0.6 %copy.10 = f32[8,16,128]{2,1,0:T(8,128)} copy(f32[8,16,128]{2,1,0:T(8,128)S(1)} %copy-done) | data formatting | bytes 131072
Async XLA Ops:
  25.5 1.5 %copy-start = (f32[8,16,128]{2,1,0:T(8,128)S(1)}, f32[8,16,128]{2,1,0:T(8,128)}, u32[]{:S(2)}) copy-start(f32[8,16,128]{2,1,0:T(8,128)} %get-tuple-element.5) | copy-start | bytes 196612

commit v4 on v3

--- a/solution.py
+++ b/solution.py
@@ -38,8 +38,7 @@
     category_in,
     table_in,
     flags_in,
-    warm_out,
-    left_out,
+    both_out,
     grid,
     basis,
     flux,
@@ -69,7 +68,7 @@
     row_recv,
 ):
     plane, line = counts[0] * counts[1], counts[2]
-    nx, ny, nz = warm_out.shape
+    nx, ny, nz = both_out.shape[1:]
     depth = ITERS + 1
     wide, tall, long = grid.shape[1:]
     short = ny + SUB
@@ -189,12 +188,6 @@
             good = one if good is None else jnp.logical_and(good, one)
         return good
 
-    z_copies = []
-    for k, dz in enumerate((1, -1)):
-        copy = remote(edges, beside.at[k], z_send.at[k], z_recv.at[k], (0, 0, dz))
-        z_copies.append((copy, dz))
-        pl.when(exists((0, 0, dz)))(copy.start)
-
     def share(stage, rows_ref, slot, targets):
         for target in targets:
             pltpu.make_async_remote_copy(
@@ -218,6 +211,14 @@
             )
             whole.wait_send()
             whole.wait_recv()
+
+    share(0, plane_rows.at[0], in_plane, plane_targets)
+
+    z_copies = []
+    for k, dz in enumerate((1, -1)):
+        copy = remote(edges, beside.at[k], z_send.at[k], z_recv.at[k], (0, 0, dz))
+        z_copies.append((copy, dz))
+        pl.when(exists((0, 0, dz)))(copy.start)
 
     def ranges(offset):
         dx, dy = offset
@@ -277,8 +278,6 @@
     for copy, (dx, dy) in raw:
         pl.when(exists((dx, dy, 0)))(copy.start)
 
-    share(0, plane_rows.at[0], in_plane, plane_targets)
-
     for copy, dz in z_copies:
         pl.when(exists((0, 0, -dz)))(copy.wait_recv)
     low_half = lane % SLOT < SLOT // 2
@@ -474,8 +473,8 @@
             if k < ITERS:
                 warm = warm + moved[k] * value
             end = end + left[k] * value
-        warm_out[i] = warm
-        left_out[i] = end
+        both_out[0, i] = warm
+        both_out[1, i] = end
 
     for copy, dz in z_copies:
         pl.when(exists((0, 0, dz)))(copy.wait_send)
@@ -493,13 +492,12 @@
     table = table[None]
     any_spec = pl.BlockSpec(memory_space=pl.ANY)
     vmem = pl.BlockSpec(memory_space=pltpu.VMEM)
-    shape = jax.ShapeDtypeStruct(warm.shape, jnp.float32)
     f32 = jnp.float32
-    return pl.pallas_call(
+    both = pl.pallas_call(
         functools.partial(kernel, counts),
-        out_shape=(shape, shape),
+        out_shape=pltpu.VMEM((2,) + warm.shape, jnp.float32),
         in_specs=[any_spec] * 5,
-        out_specs=(vmem, vmem),
+        out_specs=vmem,
         scratch_shapes=[
             pltpu.VMEM((FIELDS + 1, wide, tall, long), f32),
             pltpu.VMEM((ITERS + 1, wide, short, long), f32),
@@ -531,6 +529,7 @@
         ],
         compiler_params=pltpu.CompilerParams(collective_id=0, has_side_effects=True),
     )(warm, source, category, table, flags)
+    return both[0], both[1]
 
 
 def solution(mesh):

time: 27.9 us -> 23.3 us (0.84)
  Pallas kernels: 24.9 us -> 21.8 us
  local copies, waits for them, and re-layouts: 2.14 us -> 0.66 us
    pallas_call x1, Pallas kernels: 24.9 us -> 21.8 us  [body(): pl.pallas_call(functools.partial(kernel, counts), out_shape=pltpu.VMEM((2...]
    unnamed x4 -> x0, local copies, waits for them, and re-layouts: 2.14 us -> none
    squeeze x0 -> x1, local copies, waits for them, and re-layouts: none -> 0.66 us  [body(): return (both[0], both[1])]
where the time goes in v4:
time: 23.3 us; the launch traced here: 23.1 us
  Pallas kernels  21.8 us (94%)
  local copies, waits for them, and re-layouts  0.66 us (3%)
  between operations  0.64 us (3%)
    pallas_call x1, Pallas kernels, body(): pl.pallas_call(functools.partial(kernel, counts), out_shape=pltpu.VMEM((2...  21.8 us
    squeeze x1, local copies, waits for them, and re-layouts, body(): return (both[0], both[1])  0.66 us

profile of v4, /device:TPU:0, one launch (start us, length us, event | category | flops | bytes accessed | tf_op | source)
XLA Modules:
  0.0 23.1 jit_solution(17303898409079500478)
XLA Ops:
  0.6 21.8 %shard_map.68 = f32[2,8,16,128]{3,2,1,0:T(8,128)S(1)} custom-call(f32[8,16,128]{2,1,0:T(8,128)} %warm_in.1, f32[8,16,128]{2,1,0:T(8,128)} %source_in.1, s32[8,16,128]{2,1,0:T(8,128)} %category_in.1, f32[1,16]{1,0:T(1,128)} %bitcast.5, s32[8,16,128]{2,1,0:T(8,128)} %flags_in.1), custom_call_target="tpu_custom_call" | custom-call | tf_op jit(solution)/shard_map/pallas_call | solution.py:496
  22.4 0.7 %slice_bitcast_fusion = (f32[8,16,128]{2,1,0:T(8,128)}, f32[8,16,128]{2,1,0:T(8,128)}) fusion(f32[2,8,16,128]{3,2,1,0:T(8,128)S(1)} %shard_map.68), kind=kLoop, calls=%fused_computation | loop fusion | bytes 262144 | tf_op jit(solution)/shard_map/squeeze | solution.py:532
